TPU v7x, 32 devices: a whole 2x2x4 slice. The times are simulated.
32 devices in a mesh: grp: 4 (over y, core), seq: 8 (over z, x).
Axes of the slice: x: 2, y: 2, z: 4, core: 2. Of those that a mesh axis runs over, the one named last changes fastest.
Arguments:
- layer_input: bfloat16 [8192, 2048], P(('grp', 'seq')), may hold values from -6 to 6
- entry_gain: float32 [2048], replicated, may hold values from 0.1 to 1.9
- entry_shift: float32 [2048], replicated, may hold values from -1.75 to 1.75
- joint_weight: bfloat16 [2048, 6144], P(('grp', 'seq')), may hold values from -0.125 to 0.125
- query_offset: float32 [2048], replicated, may hold values from -3 to 3
- value_offset: float32 [2048], replicated, may hold values from -0.3125 to 0.3125
- mixing_weight: bfloat16 [2048, 2048], P(('grp', 'seq')), may hold values from -1 to 1
- attention_offset: float32 [2048], replicated, may hold values from -3 to 3
- middle_gain: float32 [2048], replicated, may hold values from 0.1 to 1.9
- middle_shift: float32 [2048], replicated, may hold values from -1.75 to 1.75
- expand_weight: bfloat16 [2048, 8192], P(('grp', 'seq')), may hold values from -0.125 to 0.125
- expand_offset: float32 [8192], replicated, may hold values from -3 to 3
- shrink_weight: bfloat16 [2048, 8192], P(('grp', 'seq')), may hold values from -0.0625 to 0.0625
- shrink_offset: float32 [2048], replicated, may hold values from -3 to 3
- placement: int32 [4, 2048], P('grp'), may hold values from 0 to 2047, each once within a row
- slot_lengths: int32 [4, 4], P('grp'), may hold values from 1 to 256, 832 in all within a row
- cotangent: bfloat16 [8192, 2048], P(('grp', 'seq')), may hold values from -6 to 6
Outputs:
- layer_output: bfloat16 [8192, 2048], P(('grp', 'seq'))
- input_gradient: bfloat16 [8192, 2048], P(('grp', 'seq'))
- entry_gain_gradient: float32 [2048], replicated
- entry_shift_gradient: float32 [2048], replicated
- joint_gradient: float32 [2048, 6144], P(('grp', 'seq'))
- query_gradient: float32 [2048], replicated
- value_gradient: float32 [2048], replicated
- mixing_gradient: float32 [2048, 2048], P(('grp', 'seq'))
- attention_offset_gradient: float32 [2048], replicated
- middle_gain_gradient: float32 [2048], replicated
- middle_shift_gradient: float32 [2048], replicated
- expand_gradient: float32 [2048, 8192], P(('grp', 'seq'))
- expand_offset_gradient: float32 [8192], replicated
- shrink_gradient: float32 [2048, 8192], P(('grp', 'seq'))
- shrink_offset_gradient: float32 [2048], replicated
Inputs may be any that keep to these rules, and one draw needn't show every extreme that they name: `placement`: each row holds every position of its group once. `slot_lengths`: the real tokens of each slot of 256 positions; the rest of a slot is padding; some slot of every group is full.
All inputs are finite; a program needn't handle non-finite values.
Results may differ from a plain program's by a relative error of at most 0.013.
Values may be sent and summed in bfloat16 or wider, within the bound.
A program may use at most 704 MiB of HBM per device.

v0:
```python
import jax
import jax.numpy as jnp
from jax import lax
from jax.sharding import Mesh, PartitionSpec as P

HEADS = 16
CONT = 256
QBLOCK = 512
PLANE = ("grp", "sub")
EVERY = ("grp", "rep", "sub")
norm_epsilon = 1e-05
masked_score = -1e30


def norm_terms(values):
    average = jnp.mean(values, axis=-1, keepdims=True)
    centered = values - average
    variance = jnp.mean(centered * centered, axis=-1, keepdims=True)
    inverse = lax.rsqrt(variance + norm_epsilon)
    return (centered * inverse, inverse)


def norm_back(slope, gain, normal, inverse):
    scaled = slope * gain
    return inverse * (
        scaled
        - jnp.mean(scaled, axis=-1, keepdims=True)
        - normal * jnp.mean(scaled * normal, axis=-1, keepdims=True)
    )


def exact_gelu(values):
    return jax.nn.gelu(values, approximate=False)


def key_bounds(positions, lengths, prompt):
    segment = (positions - prompt) // CONT
    within = positions - prompt - segment * CONT
    slot_ids = jnp.arange(lengths.shape[0], dtype=jnp.int32)
    slot_limit = jnp.sum(
        jnp.where(segment[:, None] == slot_ids[None, :], lengths[None, :], 0), axis=1
    )
    last = prompt + (segment + 1) * CONT - 1
    last = jnp.where(within < slot_limit, last, -1)
    return jnp.where(positions < prompt, positions.shape[0], last)


def block_mask(query_place, key_place, key_last):
    query_col = query_place[:, None]
    return (key_place[None, :] <= query_col) & (query_col <= key_last[None, :])


def product(left_matrix, right_matrix):
    return jnp.dot(left_matrix, right_matrix, preferred_element_type=jnp.float32)


def product_transposed(left_matrix, right_matrix):
    return lax.dot_general(
        left_matrix, right_matrix, (((1,), (1,)), ((), ())), preferred_element_type=jnp.float32
    )


def row_outer(left_matrix, right_matrix):
    return lax.dot_general(
        left_matrix, right_matrix, (((0,), (0,)), ((), ())), preferred_element_type=jnp.float32
    )


def attention_forward(grouped, places, key_last, score_scale):
    queries = grouped[:, :, 0]
    key_vectors = grouped[:, :, 1]
    values = grouped[:, :, 2]
    rows_total = grouped.shape[0]

    def one_block(block_index):
        first_row = block_index * QBLOCK
        block_queries = lax.dynamic_slice_in_dim(queries, first_row, QBLOCK, 0)
        block_places = lax.dynamic_slice_in_dim(places, first_row, QBLOCK, 0)
        allowed = block_mask(block_places, places, key_last)
        scores = (
            jnp.einsum(
                "qhe,khe->hqk", block_queries, key_vectors, preferred_element_type=jnp.float32
            )
            * score_scale
        )
        scores = jnp.where(allowed[None], scores, masked_score)
        row_top = jnp.max(scores, axis=2, keepdims=True)
        row_total = jnp.sum(jnp.exp(scores - row_top), axis=2, keepdims=True)
        log_total = row_top + jnp.log(row_total)
        soft_weights = jnp.exp(scores - log_total).astype(jnp.bfloat16)
        mixture = jnp.einsum(
            "hqk,khe->qhe", soft_weights, values, preferred_element_type=jnp.float32
        )
        return (mixture.astype(jnp.bfloat16), jnp.transpose(log_total[:, :, 0]))

    mixture, log_totals = lax.map(one_block, jnp.arange(rows_total // QBLOCK, dtype=jnp.int32))
    return (mixture.reshape(rows_total, -1), log_totals.reshape(rows_total, -1))


def attention_backward(grouped, log_totals, slopes, places, key_last, score_scale):
    queries = grouped[:, :, 0]
    key_vectors = grouped[:, :, 1]
    values = grouped[:, :, 2]
    rows_total = grouped.shape[0]

    def one_block(running, block_index):
        key_sum, value_sum = running
        first_row = block_index * QBLOCK
        block_queries = lax.dynamic_slice_in_dim(queries, first_row, QBLOCK, 0)
        block_slopes = lax.dynamic_slice_in_dim(slopes, first_row, QBLOCK, 0)
        block_totals = lax.dynamic_slice_in_dim(log_totals, first_row, QBLOCK, 0)
        block_places = lax.dynamic_slice_in_dim(places, first_row, QBLOCK, 0)
        allowed = block_mask(block_places, places, key_last)
        scores = (
            jnp.einsum(
                "qhe,khe->hqk", block_queries, key_vectors, preferred_element_type=jnp.float32
            )
            * score_scale
        )
        scores = jnp.where(allowed[None], scores, masked_score)
        probable = jnp.exp(scores - jnp.transpose(block_totals)[:, :, None])
        weight_slope = jnp.einsum(
            "qhe,khe->hqk", block_slopes, values, preferred_element_type=jnp.float32
        )
        centre = jnp.sum(probable * weight_slope, axis=2, keepdims=True)
        score_slope = (probable * (weight_slope - centre)).astype(jnp.bfloat16)
        query_slope = (
            jnp.einsum("hqk,khe->qhe", score_slope, key_vectors, preferred_element_type=jnp.float32)
            * score_scale
        )
        key_sum = (
            key_sum
            + jnp.einsum(
                "hqk,qhe->khe", score_slope, block_queries, preferred_element_type=jnp.float32
            )
            * score_scale
        )
        value_sum = value_sum + jnp.einsum(
            "hqk,qhe->khe",
            probable.astype(jnp.bfloat16),
            block_slopes,
            preferred_element_type=jnp.float32,
        )
        return ((key_sum, value_sum), query_slope)

    empty_sums = jnp.zeros(values.shape, jnp.float32)
    (key_sum, value_sum), query_slopes = lax.scan(
        one_block, (empty_sums, empty_sums), jnp.arange(rows_total // QBLOCK, dtype=jnp.int32)
    )
    query_slopes = query_slopes.reshape(values.shape)
    return jnp.stack([query_slopes, key_sum, value_sum], axis=2).astype(jnp.bfloat16)


def plane_columns(weight, plane_count):
    rows, columns = weight.shape
    own = lax.all_to_all(
        weight.reshape(rows, plane_count, columns // plane_count),
        PLANE,
        split_axis=1,
        concat_axis=0,
        tiled=True,
    ).reshape(plane_count * rows, columns // plane_count)
    every = lax.all_gather(own, "rep", axis=0, tiled=True)
    groups, reps, subs = (lax.axis_size(name) for name in EVERY)
    every = every.reshape(reps, groups, subs, rows, -1).transpose(1, 0, 2, 3, 4)
    return every.reshape(reps * groups * subs * rows, -1)


def owner_rows(gradient, plane_count):
    groups, reps, subs = (lax.axis_size(name) for name in EVERY)
    columns = gradient.shape[1]
    rows = gradient.shape[0] // (groups * reps * subs)
    ordered = gradient.astype(jnp.bfloat16).reshape(groups, reps, subs, rows, columns)
    ordered = ordered.transpose(1, 0, 2, 3, 4).reshape(-1, columns)
    summed = lax.psum_scatter(ordered, "rep", scatter_dimension=0, tiled=True)
    own = lax.all_to_all(
        summed.reshape(plane_count, rows, columns), PLANE, split_axis=0, concat_axis=0, tiled=True
    )
    return own.transpose(1, 0, 2).reshape(rows, plane_count * columns).astype(jnp.float32)


def shards(
    layer_input,
    entry_gain,
    entry_shift,
    joint_weight,
    query_offset,
    value_offset,
    mixing_weight,
    attention_offset,
    middle_gain,
    middle_shift,
    expand_weight,
    expand_offset,
    shrink_weight,
    shrink_offset,
    placement,
    slot_lengths,
    cotangent,
):
    token_rows, width = layer_input.shape
    hidden_width = expand_weight.shape[1]
    groups, reps, subs = (lax.axis_size(name) for name in EVERY)
    plane_count = groups * subs
    plane_index = lax.axis_index(PLANE)
    rep_index = lax.axis_index("rep")
    head_size = width // HEADS
    local_heads = HEADS // plane_count
    head_columns = local_heads * head_size
    score_scale = head_size ** (-0.5)
    placements = lax.all_gather(placement, "grp", axis=0, tiled=True)
    lengths_all = lax.all_gather(slot_lengths, "grp", axis=0, tiled=True)
    places = lax.dynamic_index_in_dim(placements, rep_index, 0, keepdims=False)
    lengths = lax.dynamic_index_in_dim(lengths_all, rep_index, 0, keepdims=False)
    prompt = places.shape[0] // 2
    key_last = key_bounds(places, lengths, prompt)
    joint_slice = plane_columns(joint_weight, plane_count)
    expand_slice = plane_columns(expand_weight, plane_count)
    shrink_slice = plane_columns(shrink_weight, plane_count)
    mixing_whole = lax.all_gather(mixing_weight, EVERY, axis=0, tiled=True)
    input_float = layer_input.astype(jnp.float32)
    entry_normal, entry_inverse = norm_terms(input_float)
    entry_normed = (entry_normal * entry_gain + entry_shift).astype(jnp.bfloat16)
    entry_all = lax.all_gather(entry_normed, PLANE, axis=0, tiled=True)
    plane_rows = entry_all.shape[0]
    offsets = jnp.stack(
        [
            query_offset.reshape(HEADS, head_size),
            jnp.zeros((HEADS, head_size), jnp.float32),
            value_offset.reshape(HEADS, head_size),
        ],
        axis=1,
    ).reshape(-1)
    offsets = lax.dynamic_slice_in_dim(offsets, plane_index * 3 * head_columns, 3 * head_columns)
    joint_values = (product(entry_all, joint_slice) + offsets).astype(jnp.bfloat16)
    heads_kept = lax.all_to_all(
        joint_values.reshape(groups, plane_rows // groups, 3 * head_columns),
        "rep",
        split_axis=0,
        concat_axis=0,
        tiled=True,
    ).reshape(plane_rows, local_heads, 3, head_size)
    mixture, log_totals = attention_forward(heads_kept, places, key_last, score_scale)

    def to_tokens(array):
        columns = array.shape[1]
        at_plane = lax.all_to_all(
            array.reshape(reps, plane_rows // reps, columns),
            "rep",
            split_axis=0,
            concat_axis=0,
            tiled=True,
        )
        return at_plane.reshape(plane_count, token_rows, columns)

    attended = lax.all_to_all(to_tokens(mixture), PLANE, split_axis=0, concat_axis=0, tiled=True)
    attended = attended.transpose(1, 0, 2).reshape(token_rows, width)
    residual = input_float + (product(attended, mixing_whole) + attention_offset)
    middle_normal, middle_inverse = norm_terms(residual)
    middle_normed = (middle_normal * middle_gain + middle_shift).astype(jnp.bfloat16)
    middle_all = lax.all_gather(middle_normed, PLANE, axis=0, tiled=True)
    cotangent_all = lax.all_gather(cotangent, PLANE, axis=0, tiled=True)
    hidden_local = hidden_width // plane_count
    offset_local = lax.dynamic_slice_in_dim(expand_offset, plane_index * hidden_local, hidden_local)
    expanded = product(middle_all, expand_slice) + offset_local
    activated_float, gelu_back = jax.vjp(exact_gelu, expanded)
    activated = activated_float.astype(jnp.bfloat16)
    activated_slope = product(cotangent_all, shrink_slice)
    expanded_slope = gelu_back(activated_slope)[0].astype(jnp.bfloat16)
    slope_part = product_transposed(expanded_slope, expand_slice).astype(jnp.bfloat16)
    normed_slope = lax.psum_scatter(slope_part, PLANE, scatter_dimension=0, tiled=True).astype(
        jnp.float32
    )
    output_part = product_transposed(activated, shrink_slice).astype(jnp.bfloat16)
    shrunk = lax.psum_scatter(output_part, PLANE, scatter_dimension=0, tiled=True)
    layer_output = (residual + shrunk.astype(jnp.float32) + shrink_offset).astype(jnp.bfloat16)
    cotangent_float = cotangent.astype(jnp.float32)
    residual_slope = cotangent_float + norm_back(
        normed_slope, middle_gain, middle_normal, middle_inverse
    )
    branch_slope = residual_slope.astype(jnp.bfloat16)
    attended_slope = product_transposed(branch_slope, mixing_whole).astype(jnp.bfloat16)
    slope_plane = lax.all_to_all(
        attended_slope.reshape(token_rows, plane_count, head_columns).transpose(1, 0, 2),
        PLANE,
        split_axis=0,
        concat_axis=0,
        tiled=True,
    )
    head_slopes = lax.all_to_all(
        slope_plane.reshape(groups, plane_rows // groups, head_columns),
        "rep",
        split_axis=0,
        concat_axis=0,
        tiled=True,
    ).reshape(plane_rows, local_heads, head_size)
    joint_heads = attention_backward(
        heads_kept, log_totals, head_slopes, places, key_last, score_scale
    )
    joint_slope = to_tokens(joint_heads.reshape(plane_rows, 3 * head_columns)).reshape(
        plane_rows, 3 * head_columns
    )
    entry_part = product_transposed(joint_slope, joint_slice).astype(jnp.bfloat16)
    entry_slope = lax.psum_scatter(entry_part, PLANE, scatter_dimension=0, tiled=True).astype(
        jnp.float32
    )
    input_gradient = (
        residual_slope + norm_back(entry_slope, entry_gain, entry_normal, entry_inverse)
    ).astype(jnp.bfloat16)
    slope_sums = jnp.sum(joint_slope.astype(jnp.float32), axis=0).reshape(local_heads, 3, head_size)

    def placed(piece, whole_size):
        return lax.dynamic_update_slice_in_dim(
            jnp.zeros((whole_size,), jnp.float32), piece, plane_index * piece.shape[0], 0
        )

    small_sums = lax.psum(
        (
            jnp.sum(entry_slope * entry_normal, axis=0),
            jnp.sum(entry_slope, axis=0),
            placed(slope_sums[:, 0].reshape(-1), width),
            placed(slope_sums[:, 2].reshape(-1), width),
            jnp.sum(branch_slope.astype(jnp.float32), axis=0),
            jnp.sum(normed_slope * middle_normal, axis=0),
            jnp.sum(normed_slope, axis=0),
            placed(jnp.sum(expanded_slope.astype(jnp.float32), axis=0), hidden_width),
            jnp.sum(cotangent_float, axis=0),
        ),
        EVERY,
    )
    shrink_gradient = owner_rows(row_outer(cotangent_all, activated), plane_count)
    expand_gradient = owner_rows(row_outer(middle_all, expanded_slope), plane_count)
    mixing_gradient = lax.psum_scatter(
        row_outer(attended, branch_slope).astype(jnp.bfloat16),
        EVERY,
        scatter_dimension=0,
        tiled=True,
    ).astype(jnp.float32)
    joint_gradient = owner_rows(row_outer(entry_all, joint_slope), plane_count)
    return (
        layer_output,
        input_gradient,
        small_sums[0],
        small_sums[1],
        joint_gradient,
        small_sums[2],
        small_sums[3],
        mixing_gradient,
        small_sums[4],
        small_sums[5],
        small_sums[6],
        expand_gradient,
        small_sums[7],
        shrink_gradient,
        small_sums[8],
    )


def solution(mesh):
    groups, sequence = (mesh.shape["grp"], mesh.shape["seq"])
    subs = sequence // groups
    planes = Mesh(mesh.devices.reshape(groups, sequence // subs, subs), EVERY)
    rows, whole, group_rows = (P(EVERY, None), P(), P("grp", None))
    return jax.shard_map(
        shards,
        mesh=planes,
        in_specs=(
            rows,
            whole,
            whole,
            rows,
            whole,
            whole,
            rows,
            whole,
            whole,
            whole,
            rows,
            whole,
            rows,
        )
        + (whole, group_rows, group_rows, rows),
        out_specs=(
            rows,
            rows,
            whole,
            whole,
            rows,
            whole,
            whole,
            rows,
            whole,
            whole,
            whole,
            rows,
            whole,
        )
        + (rows, whole),
        check_vma=False,
    )
```

profile of v0, /device:TPU:8, one launch (start us, length us, event | category | flops | bytes accessed | tf_op | source)
XLA Modules:
  0.0 1536.1 jit_solution(3426588837099018649)
XLA Ops:
  8.5 15.8 %all_to_all.90 = bf16[64,8,768]{2,0,1:T(8,128)(2,1)} all-to-all(bf16[64,8,768]{2,0,1:T(8,128)(2,1)S(1)} %bitcast.227), channel_id=1, replica_groups=mesh['grp'=4,'rep'=4,'sub'=2] {'grp','sub'}, dimensions={1} | all-to-all | bytes 1572864 | tf_op jit(solution)/shard_map/all_to_all | solution.py:156
  34.0 13.5 all-to-all-done.4
  51.7 33.8 %all-gather.12.cloned.1.call-done = bf16[2048,768]{1,0:T(8,128)(2,1)} async-done(((bf16[512,768]{1,0:T(8,128)(2,1)}), bf16[2048,768]{1,0:T(8,128)(2,1)}) %all-gather.12.cloned.1.call-update) | async-done | bytes 3145744 | tf_op jit(solution)/shard_map/all_gather | solution.py:163
  89.3 54.0 %all-gather.10.cloned.1.call-done = bf16[2048,2048]{1,0:T(8,128)(2,1)} async-done(((bf16[256,2048]{1,0:T(8,128)(2,1)}), bf16[2048,2048]{1,0:T(8,128)(2,1)}) %all-gather.10.cloned.1.call-update) | async-done | bytes 8388624 | tf_op jit(solution)/shard_map/all_gather | solution.py:224
  143.3 11.2 add_convert_fusion.1
  175.4 90.0 %all-to-all-done.1 = bf16[4,512,768]{1,2,0:T(8,128)(2,1)} async-done(((bf16[4,512,768]{1,2,0:T(8,128)(2,1)}), bf16[4,512,768]{1,2,0:T(8,128)(2,1)}, u32[]{:S(2)}, u32[]{:S(2)}) %all-to-all-start.1) | async-done | bytes 3145760 | tf_op jit(solution)/shard_map/all_to_all | solution.py:236
  284.3 53.2 %while.27 = (s32[]{:T(128)}, bf16[4,512,2,128]{1,3,2,0:T(8,128)(2,1)}, f32[4,512,2]{1,2,0:T(2,128)}, s32[2048]{0:T(1024)S(1)}, s32[4]{0:T(128)S(1)}, /*index=5*/...) while((s32[]{:T(128)}, ...), condition=%wide.region_6.7_spmd, body=%wide.region_3.6_spmd.sunk | while | flops 1100086272 | bytes 33086656 | solution.py:96
  337.5 36.7 %all_to_all.91 = bf16[4,512,256]{1,2,0:T(8,128)(2,1)} all-to-all(bf16[4,512,256]{1,2,0:T(8,128)(2,1)} %bitcast.238), channel_id=1, replica_groups=mesh['grp'=4,'rep'=4,'sub'=2] {'rep'}, dimensions={0} | all-to-all | bytes 2097152 | tf_op jit(solution)/shard_map/all_to_all | solution.py:247
  376.5 19.1 %all_to_all.92 = bf16[8,256,256]{2,1,0:T(8,128)(2,1)} all-to-all(bf16[8,256,256]{2,1,0:T(8,128)(2,1)} %bitcast.217), channel_id=1, replica_groups=mesh['grp'=4,'rep'=4,'sub'=2] {'grp','sub'}, dimensions={0} | all-to-all | bytes 2097152 | tf_op jit(solution)/shard_map/all_to_all | solution.py:256
  414.1 30.0 %all-gather.20.cloned.1.call-done = bf16[2048,1024]{1,0:T(8,128)(2,1)} async-done(((bf16[512,1024]{1,0:T(8,128)(2,1)}), bf16[2048,1024]{1,0:T(8,128)(2,1)}) %all-gather.20.cloned.1.call-update) | async-done | bytes 4194320 | tf_op jit(solution)/shard_map/all_gather | solution.py:163
  449.0 53.0 %all-gather.16.cloned.1.call-done = bf16[2048,2048]{1,0:T(8,128)(2,1)} async-done(((bf16[256,2048]{1,0:T(8,128)(2,1)}), bf16[2048,2048]{1,0:T(8,128)(2,1)}) %all-gather.16.cloned.1.call-update) | async-done | bytes 8388624 | tf_op jit(solution)/shard_map/all_gather | solution.py:261
  502.0 14.4 fusion.70
  516.5 41.9 %all-gather.22.cloned.1.call-done = bf16[2048,2048]{1,0:T(8,128)(2,1)} async-done(((bf16[256,2048]{1,0:T(8,128)(2,1)}), bf16[2048,2048]{1,0:T(8,128)(2,1)}) %all-gather.22.cloned.1.call-update) | async-done | bytes 8388624 | tf_op jit(solution)/shard_map/all_gather | solution.py:262
  558.3 33.5 %convert_reduce_fusion = (f32[1024]{0:T(1024)}, bf16[2048,1024]{1,0:T(8,128)(2,1)S(1)}, f32[2048,1024]{1,0:T(8,128)}) fusion(f32[2048,1024]{1,0:T(8,128)} %fusion.70, f32[1024]{0:T(1024)S(1)} %dynamic_slice.42, bf16[2048,2048]{1,0:T(8,128)(2,1)} %all-gather.22.cloned.1.call-done, bf16[2048,1024]{1,0:T(8,128)(2,1)} %bitcast.207), kind=kOutput, calls=%fused_computation.46 | convolution fusion | flops 8747219968 | bytes 33562624 | tf_op jit(solution)/shard_map/dot_general | solution.py:54
  593.8 11.1 convolution_convert_fusion.2
  605.0 10.6 multiply_convert_fusion.1
  615.6 14.2 convolution_convert_fusion.3
  629.9 13.3 convolution_convert_fusion.4
  645.7 30.6 %reduce-scatter.10.cloned.1.call-done = bf16[256,2048]{1,0:T(8,128)(2,1)} async-done(((bf16[2048,2048]{1,0:T(8,128)(2,1)}), bf16[256,2048]{1,0:T(8,128)(2,1)}) %reduce-scatter.10.cloned.1.call-update) | async-done | bytes 1048592 | tf_op jit(solution)/shard_map/reduce_scatter | solution.py:271
  679.1 72.3 %reduce-scatter.8.cloned.1.call-done = bf16[256,2048]{1,0:T(8,128)(2,1)} async-done(((bf16[2048,2048]{1,0:T(8,128)(2,1)}), bf16[256,2048]{1,0:T(8,128)(2,1)}) %reduce-scatter.8.cloned.1.call-update) | async-done | bytes 1048592 | tf_op jit(solution)/shard_map/reduce_scatter | solution.py:275
  768.1 14.9 all-to-all-done.6
  788.2 14.1 convert_bitcast_fusion
  813.6 26.1 %all-to-all-done.7 = bf16[4,512,256]{2,1,0:T(8,128)(2,1)S(1)} async-done(((bf16[4,512,256]{2,1,0:T(8,128)(2,1)}), bf16[4,512,256]{2,1,0:T(8,128)(2,1)S(1)}, u32[]{:S(2)}, u32[]{:S(2)}) %all-to-all-start.7) | async-done | bytes 1048608 | tf_op jit(solution)/shard_map/all_to_all | solution.py:290
  841.1 112.7 %while.28 = (s32[]{:T(128)}, f32[2048,2,128]{0,2,1:T(8,128)}, f32[2048,2,128]{0,2,1:T(8,128)}, bf16[4,512,2,128]{3,1,0,2:T(8,128)(2,1)}, s32[4]{0:T(128)S(1)}, /...) while((s32[]{:T(128)}, f32[2048,2,128]{0,2,1:T(8,128)}, ...), condition=%wide.region_15.16_spmd.clone, body=%wide.region_13.15_spmd.clone.sunk | while | flops 2721709056 | bytes 147901232 | solution.py:147
  968.3 73.6 %all_to_all.93 = bf16[4,512,768]{1,2,0:T(8,128)(2,1)S(1)} all-to-all(bf16[4,512,768]{1,2,0:T(8,128)(2,1)S(1)} %copy.180), channel_id=1, replica_groups=mesh['grp'=4,'rep'=4,'sub'=2] {'rep'}, dimensions={0} | all-to-all | bytes 6291456 | tf_op jit(solution)/shard_map/all_to_all | solution.py:247
  1064.2 11.4 convolution_convert_fusion.1
  1079.3 14.8 all-to-all-done.10
  1102.0 11.6 all-to-all-done.11
  1126.2 17.7 %all-to-all-done.9 = bf16[8,64,768]{2,1,0:T(8,128)(2,1)} async-done(((bf16[8,64,768]{2,1,0:T(8,128)(2,1)}), bf16[8,64,768]{2,1,0:T(8,128)(2,1)}, u32[]{:S(2)}, u32[]{:S(2)}) %all-to-all-start.9) | async-done | bytes 786464 | tf_op jit(solution)/shard_map/all_to_all | solution.py:176
  1146.5 161.7 %reduce-scatter.16.cloned.1.call-done = bf16[64,2048]{1,0:T(8,128)(2,1)} async-done(((bf16[2048,2048]{1,0:T(8,128)(2,1)}), bf16[64,2048]{1,0:T(8,128)(2,1)}) %reduce-scatter.16.cloned.1.call-update) | async-done | bytes 262160 | tf_op jit(solution)/shard_map/reduce_scatter | solution.py:333
  1310.0 72.0 %reduce-scatter.12.cloned.1.call-done = bf16[256,2048]{1,0:T(8,128)(2,1)} async-done(((bf16[2048,2048]{1,0:T(8,128)(2,1)}), bf16[256,2048]{1,0:T(8,128)(2,1)}) %reduce-scatter.12.cloned.1.call-update) | async-done | bytes 1048592 | tf_op jit(solution)/shard_map/reduce_scatter | solution.py:304
  1388.0 129.6 %all-reduce.3.cloned.1.call-done = (f32[2048]{0:T(1024)}, f32[2048]{0:T(1024)}, f32[2048]{0:T(1024)}, f32[2048]{0:T(1024)}, f32[2048]{0:T(1024)}, /*index=5*/f32...) async-done(((f32[2048]{0:T(1024)}, f32[2048]{0:T(1024)}, f32[2048]{0:T(1024)}, f32[2048]{0:T(1024)}, f32[2048]{0:T(1024)}, /*index=5*/f32[2048]{0:T(1024)}, ...) | async-done | bytes 98320 | tf_op jit(solution)/shard_map/psum | solution.py:317
  (332 shorter events, 369.1 us)
Async XLA Ops:
  7.2 78.3 %all-gather.12.cloned.1.call-start = ((), (), s32[]{:S(2)}) async-start(), calls=%async_computation.20 | async-start | bytes 3932160 | tf_op jit(solution)/shard_map/all_gather | solution.py:163
  24.4 118.9 %all-gather.10.cloned.1.call-start = ((), (), s32[]{:S(2)}) async-start(), calls=%async_computation.19 | async-start | bytes 9437184 | tf_op jit(solution)/shard_map/all_gather | solution.py:224
  27.3 370.6 %all-gather.14.cloned.1.call-start = ((), (), s32[]{:S(2)}) async-start(), calls=%async_computation.21 | async-start | bytes 8650752 | tf_op jit(solution)/shard_map/all_gather | solution.py:220
  29.1 18.4 %all-to-all-start.4 = ((bf16[64,8,1024]{2,0,1:T(8,128)(2,1)}), bf16[64,8,1024]{2,0,1:T(8,128)(2,1)S(1)}, u32[]{:S(2)}, u32[]{:S(2)}) async-start(bf16[64,8,1024]{2,0,1:T(8,128)(2,1)} %bitcast.167), calls=%async_computation.4 | async-start | bytes 2097152 | tf_op jit(solution)/shard_map/all_to_all | solution.py:156
  47.5 111.7 %all-to-all-start.5 = ((bf16[64,8,1024]{2,0,1:T(8,128)(2,1)}), bf16[64,8,1024]{2,0,1:T(8,128)(2,1)S(1)}, u32[]{:S(2)}, u32[]{:S(2)}) async-start(bf16[64,8,1024]{2,0,1:T(8,128)(2,1)} %bitcast.214), calls=%async_computation.5 | async-start | bytes 2097152 | tf_op jit(solution)/shard_map/all_to_all | solution.py:156
  51.1 358.1 %all-gather.18.cloned.1.call-start = ((), (), s32[]{:S(2)}) async-start(), calls=%async_computation.23 | async-start | bytes 5242880 | tf_op jit(solution)/shard_map/all_gather | solution.py:163
  159.3 106.1 %all-to-all-start.1 = ((bf16[4,512,768]{1,2,0:T(8,128)(2,1)}), bf16[4,512,768]{1,2,0:T(8,128)(2,1)}, u32[]{:S(2)}, u32[]{:S(2)}) async-start(bf16[4,512,768]{1,2,0:T(8,128)(2,1)} %copy.159), calls=%async_computation.1 | async-start | bytes 6291456 | tf_op jit(solution)/shard_map/all_to_all | solution.py:236
  164.5 279.6 %all-gather.20.cloned.1.call-start = ((), (), s32[]{:S(2)}) async-start(), calls=%async_computation.24 | async-start | bytes 5242880 | tf_op jit(solution)/shard_map/all_gather | solution.py:163
  174.8 327.2 %all-gather.16.cloned.1.call-start = ((), (), s32[]{:S(2)}) async-start(), calls=%async_computation.22 | async-start | bytes 9437184 | tf_op jit(solution)/shard_map/all_gather | solution.py:261
  337.5 60.4 %copy-start.43 = (f32[2048]{0:T(1024)S(1)}, f32[2048]{0:T(1024)}, u32[]{:S(2)}) copy-start(f32[2048]{0:T(1024)} %param.28) | copy-start | bytes 24580
  407.6 150.8 %all-gather.22.cloned.1.call-start = ((), (), s32[]{:S(2)}) async-start(), calls=%async_computation.26 | async-start | bytes 9437184 | tf_op jit(solution)/shard_map/all_gather | solution.py:262
  408.3 268.0 %reduce-scatter.10.cloned.1.call-start = ((), (), s32[]{:S(2)}) async-start(), calls=%async_computation.27 | async-start | bytes 9437184 | tf_op jit(solution)/shard_map/reduce_scatter | solution.py:271
  604.9 146.6 %reduce-scatter.8.cloned.1.call-start = ((), (), s32[]{:S(2)}) async-start(), calls=%async_computation.25 | async-start | bytes 9437184 | tf_op jit(solution)/shard_map/reduce_scatter | solution.py:275
  629.8 445.9 %reduce-scatter.18.cloned.1.call-start = ((), (), s32[]{:S(2)}) async-start(), calls=%async_computation.31 | async-start | bytes 5242880 | tf_op jit(solution)/shard_map/reduce_scatter | solution.py:175
  645.6 105.9 %copy-start.20 = (bf16[256,2048]{1,0:T(8,128)(2,1)S(1)}, bf16[256,2048]{1,0:T(8,128)(2,1)}, u32[]{:S(2)}) copy-start(bf16[256,2048]{1,0:T(8,128)(2,1)} %param.37) | copy-start | bytes 3145732
  645.6 105.8 %copy-start.48 = (f32[2048]{0:T(1024)S(1)}, f32[2048]{0:T(1024)}, u32[]{:S(2)}) copy-start(f32[2048]{0:T(1024)} %param.34) | copy-start | bytes 24580
  763.8 19.2 %all-to-all-start.6 = ((bf16[8,256,256]{2,1,0:T(8,128)(2,1)}), bf16[8,256,256]{2,1,0:T(8,128)(2,1)}, u32[]{:S(2)}, u32[]{:S(2)}) async-start(bf16[8,256,256]{2,1,0:T(8,128)(2,1)} %bitcast.165), calls=%async_computation.8 | async-start | bytes 2097152 | tf_op jit(solution)/shard_map/all_to_all | solution.py:283
  783.0 56.7 %all-to-all-start.7 = ((bf16[4,512,256]{2,1,0:T(8,128)(2,1)}), bf16[4,512,256]{2,1,0:T(8,128)(2,1)S(1)}, u32[]{:S(2)}, u32[]{:S(2)}) async-start(bf16[4,512,256]{2,1,0:T(8,128)(2,1)} %bitcast.41), calls=%async_computation.9 | async-start | bytes 2097152 | tf_op jit(solution)/shard_map/all_to_all | solution.py:290
  788.1 291.2 %reduce-scatter.20.cloned.1.call-start = ((), (), s32[]{:S(2)}) async-start(), calls=%async_computation.32 | async-start | bytes 5242880 | tf_op jit(solution)/shard_map/reduce_scatter | solution.py:175
  813.6 303.4 %reduce-scatter.14.cloned.1.call-start = ((), (), s32[]{:S(2)}) async-start(), calls=%async_computation.29 | async-start | bytes 3932160 | tf_op jit(solution)/shard_map/reduce_scatter | solution.py:175
  1057.4 250.7 %reduce-scatter.16.cloned.1.call-start = ((), (), s32[]{:S(2)}) async-start(), calls=%async_computation.30 | async-start | bytes 8650752 | tf_op jit(solution)/shard_map/reduce_scatter | solution.py:333
  1064.2 317.8 %reduce-scatter.12.cloned.1.call-start = ((), (), s32[]{:S(2)}) async-start(), calls=%async_computation.28 | async-start | bytes 9437184 | tf_op jit(solution)/shard_map/reduce_scatter | solution.py:304
  1075.7 18.4 %all-to-all-start.10 = ((bf16[8,64,1024]{2,1,0:T(8,128)(2,1)}), bf16[8,64,1024]{2,1,0:T(8,128)(2,1)S(1)}, u32[]{:S(2)}, u32[]{:S(2)}) async-start(bf16[8,64,1024]{2,1,0:T(8,128)(2,1)} %bitcast.236), calls=%async_computation.16 | async-start | bytes 2097152 | tf_op jit(solution)/shard_map/all_to_all | solution.py:176
  1095.1 18.4 %all-to-all-start.11 = ((bf16[8,64,1024]{2,1,0:T(8,128)(2,1)}), bf16[8,64,1024]{2,1,0:T(8,128)(2,1)S(1)}, u32[]{:S(2)}, u32[]{:S(2)}) async-start(bf16[8,64,1024]{2,1,0:T(8,128)(2,1)} %bitcast.237), calls=%async_computation.18 | async-start | bytes 2097152 | tf_op jit(solution)/shard_map/all_to_all | solution.py:176
  1116.9 27.0 %all-to-all-start.9 = ((bf16[8,64,768]{2,1,0:T(8,128)(2,1)}), bf16[8,64,768]{2,1,0:T(8,128)(2,1)}, u32[]{:S(2)}, u32[]{:S(2)}) async-start(bf16[8,64,768]{2,1,0:T(8,128)(2,1)} %bitcast.242), calls=%async_computation.13 | async-start | bytes 1572864 | tf_op jit(solution)/shard_map/all_to_all | solution.py:176
  1121.1 396.4 %all-reduce.3.cloned.1.call-start = ((), (), s32[]{:S(2)}) async-start(), calls=%async_computation.33 | async-start | bytes 196608 | tf_op jit(solution)/shard_map/psum | solution.py:317
  1122.9 259.1 %copy-start.10 = (bf16[256,2048]{1,0:T(8,128)(2,1)S(1)}, bf16[256,2048]{1,0:T(8,128)(2,1)}, u32[]{:S(2)}) copy-start(bf16[256,2048]{1,0:T(8,128)(2,1)} %param.21) | copy-start | bytes 3145732
  1122.9 259.1 %copy-start.29 = (f32[2048]{0:T(1024)S(1)}, f32[2048]{0:T(1024)}, u32[]{:S(2)}) copy-start(f32[2048]{0:T(1024)} %param.22) | copy-start | bytes 24580
  1122.9 259.1 %copy-start.35 = (f32[256]{0:T(256)S(1)}, f32[256]{0:T(256)}, u32[]{:S(2)}) copy-start(f32[256]{0:T(256)} %copy-done.34) | copy-start | bytes 3076
  1122.9 259.1 %copy-start.39 = (f32[256]{0:T(256)S(1)}, f32[256]{0:T(256)}, u32[]{:S(2)}) copy-start(f32[256]{0:T(256)} %copy-done.38) | copy-start | bytes 3076
  1126.0 259.0 %copy-start.33 = (f32[2048]{0:T(1024)}, f32[2048]{0:T(1024)S(1)}, u32[]{:S(2)}) copy-start(f32[2048]{0:T(1024)S(1)} %dynamic_update_slice.21) | copy-start | bytes 24580
  1126.2 258.7 %copy-start.32 = (f32[2048]{0:T(1024)}, f32[2048]{0:T(1024)S(1)}, u32[]{:S(2)}) copy-start(f32[2048]{0:T(1024)S(1)} %dynamic_update_slice.22) | copy-start | bytes 24580
  (49 other events, 806.5 us)
Sparse Core Ops, SparseCore 0:
  24.5 60.9 all-gather.11
  87.9 55.3 all-gather.9
  146.3 122.2 all-gather.13
  270.6 84.9 all-gather.17
  357.0 87.0 all-gather.19
  446.4 55.5 all-gather.15
  503.9 54.3 all-gather.21
  605.0 71.2 reduce-scatter.9
  680.2 71.2 reduce-scatter.7
  753.6 99.2 reduce-scatter.17
  855.3 75.8 reduce-scatter.19
  1057.6 59.3 reduce-scatter.13
  1119.2 188.9 reduce-scatter.15
  1311.5 70.4 reduce-scatter.11
  1390.6 126.9 all-reduce.2
where the time goes:
time: 1540 us
  waiting for transfers between devices  873 us (57%)
  matrix products  256 us (17%)
  blocking collectives  155 us (10%)
  local copies, waits for them, and re-layouts  124 us (8%)
  other arithmetic  72.8 us (5%)
  starting transfers between devices  34.3 us (2%)
    reduce_scatter x1, waiting for transfers between devices, shards(): lax.psum_scatter(row_outer(attended, branch_slope).astype(jnp.bfloat16),...  162 us
    psum x1, waiting for transfers between devices, shards(): lax.psum((jnp.sum(entry_slope * entry_normal, axis=0), jnp.sum(entry_slop...  130 us
    all_to_all x2, blocking collectives, to_tokens(): lax.all_to_all(array.reshape(reps, plane_rows // reps, columns), 'rep', s...  110 us
    all_to_all x1, waiting for transfers between devices, shards(): lax.all_to_all(joint_values.reshape(groups, plane_rows // groups, 3 * hea...  90 us
    reduce_scatter x1, waiting for transfers between devices, shards(): lax.psum_scatter(output_part, PLANE, scatter_dimension=0, tiled=True)  72.3 us
    reduce_scatter x1, waiting for transfers between devices, shards(): lax.psum_scatter(entry_part, PLANE, scatter_dimension=0, tiled=True)  72 us
    dot_general x4, matrix products, product(): jnp.dot(left_matrix, right_matrix, preferred_element_type=jnp.float32)  65.4 us
    all_gather x3, waiting for transfers between devices, plane_columns(): every = lax.all_gather(own, 'rep', axis=0, tiled=True)  63.8 us
  transfers between devices with their start and end apart: 23, of which 18 were waited for; matrix products, arithmetic and copies ran while one was open for 25% of the time, Pallas kernels for 0%

commit v1 on v0

--- a/solution.py
+++ b/solution.py
@@ -2,6 +2,7 @@
 import jax.numpy as jnp
 from jax import lax
 from jax.sharding import Mesh, PartitionSpec as P
+from jax.lax import all_gather
 
 HEADS = 16
 CONT = 256
@@ -198,6 +199,15 @@
     slot_lengths,
     cotangent,
 ):
+
+    def produce_corner(sheet, row_data, mesh_name):
+        field_out = jnp.split(
+            all_gather(jnp.concatenate([row_data, sheet], axis=1), mesh_name, axis=0, tiled=True),
+            [row_data.shape[1]],
+            axis=1,
+        )
+        return field_out
+
     token_rows, width = layer_input.shape
     hidden_width = expand_weight.shape[1]
     groups, reps, subs = (lax.axis_size(name) for name in EVERY)
@@ -258,8 +268,7 @@
     residual = input_float + (product(attended, mixing_whole) + attention_offset)
     middle_normal, middle_inverse = norm_terms(residual)
     middle_normed = (middle_normal * middle_gain + middle_shift).astype(jnp.bfloat16)
-    middle_all = lax.all_gather(middle_normed, PLANE, axis=0, tiled=True)
-    cotangent_all = lax.all_gather(cotangent, PLANE, axis=0, tiled=True)
+    middle_all, cotangent_all = produce_corner(cotangent, middle_normed, PLANE)
     hidden_local = hidden_width // plane_count
     offset_local = lax.dynamic_slice_in_dim(expand_offset, plane_index * hidden_local, hidden_local)
     expanded = product(middle_all, expand_slice) + offset_local

time: 1540 us -> 1540 us (level)
    all_gather x2 -> x1, waiting for transfers between devices: 94.9 us -> 88.4 us  [produce_corner(): all_gather(jnp.concatenate([row_data, sheet], axis=1), mesh_name, axis=0,...]
  transfers between devices with their start and end apart: 23 -> 22, of which waited for: 18 -> 17; matrix products, arithmetic and copies ran while one was open for 25% -> 23% of each run, Pallas kernels for 0% -> 0%
where the time goes in v1:
time: 1540 us; the launch traced here: 1530 us
  waiting for transfers between devices  887 us (58%)
  matrix products  262 us (17%)
  blocking collectives  156 us (10%)
  local copies, waits for them, and re-layouts  113 us (7%)
  other arithmetic  62.6 us (4%)
  starting transfers between devices  33.7 us (2%)
    reduce_scatter x1, waiting for transfers between devices, shards(): lax.psum_scatter(row_outer(attended, branch_slope).astype(jnp.bfloat16),...  160 us
    psum x1, waiting for transfers between devices, shards(): lax.psum((jnp.sum(entry_slope * entry_normal, axis=0), jnp.sum(entry_slop...  130 us
    all_to_all x2, blocking collectives, to_tokens(): lax.all_to_all(array.reshape(reps, plane_rows // reps, columns), 'rep', s...  110 us
    all_to_all x1, waiting for transfers between devices, shards(): lax.all_to_all(joint_values.reshape(groups, plane_rows // groups, 3 * hea...  90.4 us
    all_gather x1, waiting for transfers between devices, produce_corner(): all_gather(jnp.concatenate([row_data, sheet], axis=1), mesh_name, axis=0,...  88.4 us
    reduce_scatter x1, waiting for transfers between devices, shards(): lax.psum_scatter(entry_part, PLANE, scatter_dimension=0, tiled=True)  72.8 us
    reduce_scatter x1, waiting for transfers between devices, shards(): lax.psum_scatter(output_part, PLANE, scatter_dimension=0, tiled=True)  72.3 us
    dot_general x4, matrix products, product(): jnp.dot(left_matrix, right_matrix, preferred_element_type=jnp.float32)  70.2 us
  transfers between devices with their start and end apart: 22, of which 17 were waited for; matrix products, arithmetic and copies ran while one was open for 23% of the time, Pallas kernels for 0%

profile of v1, /device:TPU:8, one launch (start us, length us, event | category | flops | bytes accessed | tf_op | source)
XLA Modules:
  0.0 1534.6 jit_solution(5985623458741168601)
XLA Ops:
  8.5 15.8 %all_to_all.90 = bf16[64,8,768]{2,0,1:T(8,128)(2,1)} all-to-all(bf16[64,8,768]{2,0,1:T(8,128)(2,1)S(1)} %bitcast.221), channel_id=1, replica_groups=mesh['grp'=4,'rep'=4,'sub'=2] {'grp','sub'}, dimensions={1} | all-to-all | bytes 1572864 | tf_op jit(solution)/shard_map/all_to_all | solution.py:157
  34.0 13.5 all-to-all-done.4
  51.6 33.9 %all-gather.11.cloned.1.call-done = bf16[2048,768]{1,0:T(8,128)(2,1)} async-done(((bf16[512,768]{1,0:T(8,128)(2,1)}), bf16[2048,768]{1,0:T(8,128)(2,1)}) %all-gather.11.cloned.1.call-update) | async-done | bytes 3145744 | tf_op jit(solution)/shard_map/all_gather | solution.py:164
  89.4 54.0 %all-gather.9.cloned.1.call-done = bf16[2048,2048]{1,0:T(8,128)(2,1)} async-done(((bf16[256,2048]{1,0:T(8,128)(2,1)}), bf16[2048,2048]{1,0:T(8,128)(2,1)}) %all-gather.9.cloned.1.call-update) | async-done | bytes 8388624 | tf_op jit(solution)/shard_map/all_gather | solution.py:234
  143.3 11.2 add_convert_fusion.1
  175.0 90.4 %all-to-all-done.1 = bf16[4,512,768]{1,2,0:T(8,128)(2,1)} async-done(((bf16[4,512,768]{1,2,0:T(8,128)(2,1)}), bf16[4,512,768]{1,2,0:T(8,128)(2,1)}, u32[]{:S(2)}, u32[]{:S(2)}) %all-to-all-start.1) | async-done | bytes 3145760 | tf_op jit(solution)/shard_map/all_to_all | solution.py:246
  284.3 53.2 %while.27 = (s32[]{:T(128)}, bf16[4,512,2,128]{1,3,2,0:T(8,128)(2,1)}, f32[4,512,2]{1,2,0:T(2,128)}, s32[2048]{0:T(1024)S(1)}, s32[4]{0:T(128)S(1)}, /*index=5*/...) while((s32[]{:T(128)}, ...), condition=%wide.region_6.7_spmd, body=%wide.region_3.6_spmd.sunk | while | flops 1100086272 | bytes 33086656 | solution.py:97
  337.6 36.6 %all_to_all.91 = bf16[4,512,256]{1,2,0:T(8,128)(2,1)} all-to-all(bf16[4,512,256]{1,2,0:T(8,128)(2,1)} %bitcast.232), channel_id=1, replica_groups=mesh['grp'=4,'rep'=4,'sub'=2] {'rep'}, dimensions={0} | all-to-all | bytes 2097152 | tf_op jit(solution)/shard_map/all_to_all | solution.py:257
  376.5 19.3 %all_to_all.92 = bf16[8,256,256]{2,1,0:T(8,128)(2,1)} all-to-all(bf16[8,256,256]{2,1,0:T(8,128)(2,1)} %bitcast.211), channel_id=1, replica_groups=mesh['grp'=4,'rep'=4,'sub'=2] {'grp','sub'}, dimensions={0} | all-to-all | bytes 2097152 | tf_op jit(solution)/shard_map/all_to_all | solution.py:266
  414.0 30.1 %all-gather.19.cloned.1.call-done = bf16[2048,1024]{1,0:T(8,128)(2,1)} async-done(((bf16[512,1024]{1,0:T(8,128)(2,1)}), bf16[2048,1024]{1,0:T(8,128)(2,1)}) %all-gather.19.cloned.1.call-update) | async-done | bytes 4194320 | tf_op jit(solution)/shard_map/all_gather | solution.py:164
  449.0 88.4 %all-gather.15.cloned.1.call-done = bf16[2048,4096]{1,0:T(8,128)(2,1)} async-done(((bf16[256,4096]{1,0:T(8,128)(2,1)}), bf16[2048,4096]{1,0:T(8,128)(2,1)}) %all-gather.15.cloned.1.call-update) | async-done | bytes 16777232 | tf_op jit(solution)/shard_map/all_gather | solution.py:205
  537.5 31.8 %multiply_convert_fusion.1 = (bf16[2048,1024]{1,0:T(8,128)(2,1)}, f32[2048,1024]{1,0:T(8,128)}, f32[2048,1024]{1,0:T(8,128)}) fusion(f32[1024]{0:T(1024)S(1)} %dynamic_slice.42, bf16[2048,1024]{1,0:T(8,128)(2,1)} %bitcast.202, bf16[2048,4096]{1,0:T(8,128)(2,1)} %all-gather.15.cloned.1.call-done), kind=kOutput, calls=%fused_computation.48 | convolution fusion | flops 8728346624 | bytes 33558528 | tf_op jit(solution)/shard_map/dot_general | solution.py:55
  569.3 20.9 %convert_reduce_fusion = (f32[1024]{0:T(1024)}, bf16[2048,1024]{1,0:T(8,128)(2,1)}) fusion(f32[2048,1024]{1,0:T(8,128)} %get-tuple-element.340, bf16[2048,1024]{1,0:T(8,128)(2,1)S(1)} %bitcast.201, bf16[2048,4096]{1,0:T(8,128)(2,1)} %all-gather.15.cloned.1.call-done, f32[2048,1024]{1,0:T(8,128)} %get-tuple-element.354, f32[1024]{0:T(1024)S(1)} %dynamic_slice.42), kind=kOutput, calls=%fused_computation.46 | convolution fusion | flops 8625585152 | bytes 33562624 | tf_op jit(solution)/shard_map/dot_general | solution.py:55
  590.2 13.4 convolution_convert_fusion.2
  603.7 14.4 convolution_convert_fusion.3
  618.2 13.3 fusion.50
  634.1 41.0 %reduce-scatter.10.cloned.1.call-done = bf16[256,2048]{1,0:T(8,128)(2,1)} async-done(((bf16[2048,2048]{1,0:T(8,128)(2,1)}), bf16[256,2048]{1,0:T(8,128)(2,1)}) %reduce-scatter.10.cloned.1.call-update) | async-done | bytes 1048592 | tf_op jit(solution)/shard_map/reduce_scatter | solution.py:280
  677.9 72.3 %reduce-scatter.8.cloned.1.call-done = bf16[256,2048]{1,0:T(8,128)(2,1)} async-done(((bf16[2048,2048]{1,0:T(8,128)(2,1)}), bf16[256,2048]{1,0:T(8,128)(2,1)}) %reduce-scatter.8.cloned.1.call-update) | async-done | bytes 1048592 | tf_op jit(solution)/shard_map/reduce_scatter | solution.py:284
  754.8 6.6 convolution_convert_fusion.5
  766.7 14.9 all-to-all-done.6
  786.8 13.1 fusion.53
  802.5 35.6 %all-to-all-done.7 = bf16[4,512,256]{2,1,0:T(8,128)(2,1)S(1)} async-done(((bf16[4,512,256]{2,1,0:T(8,128)(2,1)}), bf16[4,512,256]{2,1,0:T(8,128)(2,1)S(1)}, u32[]{:S(2)}, u32[]{:S(2)}) %all-to-all-start.7) | async-done | bytes 1048608 | tf_op jit(solution)/shard_map/all_to_all | solution.py:299
  839.2 112.5 %while.28 = (s32[]{:T(128)}, f32[2048,2,128]{0,2,1:T(8,128)}, f32[2048,2,128]{0,2,1:T(8,128)}, bf16[4,512,2,128]{3,1,0,2:T(8,128)(2,1)}, s32[4]{0:T(128)S(1)}, /...) while((s32[]{:T(128)}, f32[2048,2,128]{0,2,1:T(8,128)}, ...), condition=%wide.region_15.16_spmd.clone, body=%wide.region_13.15_spmd.clone.sunk | while | flops 2721709056 | bytes 147901232 | solution.py:148
  966.3 73.8 %all_to_all.93 = bf16[4,512,768]{1,2,0:T(8,128)(2,1)S(1)} all-to-all(bf16[4,512,768]{1,2,0:T(8,128)(2,1)S(1)} %copy.176), channel_id=1, replica_groups=mesh['grp'=4,'rep'=4,'sub'=2] {'rep'}, dimensions={0} | all-to-all | bytes 6291456 | tf_op jit(solution)/shard_map/all_to_all | solution.py:257
  1043.3 10.2 convolution_convert_fusion.4
  1062.3 11.4 convolution_convert_fusion.1
  1077.4 14.8 all-to-all-done.10
  1100.1 11.6 all-to-all-done.11
  1124.4 18.6 %all-to-all-done.9 = bf16[8,64,768]{2,1,0:T(8,128)(2,1)} async-done(((bf16[8,64,768]{2,1,0:T(8,128)(2,1)}), bf16[8,64,768]{2,1,0:T(8,128)(2,1)}, u32[]{:S(2)}, u32[]{:S(2)}) %all-to-all-start.9) | async-done | bytes 786464 | tf_op jit(solution)/shard_map/all_to_all | solution.py:177
  1145.6 160.4 %reduce-scatter.16.cloned.1.call-done = bf16[64,2048]{1,0:T(8,128)(2,1)} async-done(((bf16[2048,2048]{1,0:T(8,128)(2,1)}), bf16[64,2048]{1,0:T(8,128)(2,1)}) %reduce-scatter.16.cloned.1.call-update) | async-done | bytes 262160 | tf_op jit(solution)/shard_map/reduce_scatter | solution.py:342
  1307.8 72.8 %reduce-scatter.12.cloned.1.call-done = bf16[256,2048]{1,0:T(8,128)(2,1)} async-done(((bf16[2048,2048]{1,0:T(8,128)(2,1)}), bf16[256,2048]{1,0:T(8,128)(2,1)}) %reduce-scatter.12.cloned.1.call-update) | async-done | bytes 1048592 | tf_op jit(solution)/shard_map/reduce_scatter | solution.py:313
  1386.6 129.6 %all-reduce.3.cloned.1.call-done = (f32[2048]{0:T(1024)}, f32[2048]{0:T(1024)}, f32[2048]{0:T(1024)}, f32[2048]{0:T(1024)}, f32[2048]{0:T(1024)}, /*index=5*/f32...) async-done(((f32[2048]{0:T(1024)}, f32[2048]{0:T(1024)}, f32[2048]{0:T(1024)}, f32[2048]{0:T(1024)}, f32[2048]{0:T(1024)}, /*index=5*/f32[2048]{0:T(1024)}, ...) | async-done | bytes 98320 | tf_op jit(solution)/shard_map/psum | solution.py:326
  (328 shorter events, 340.6 us)
Async XLA Ops:
  7.2 78.3 %all-gather.11.cloned.1.call-start = ((), (), s32[]{:S(2)}) async-start(), calls=%async_computation.20 | async-start | bytes 3932160 | tf_op jit(solution)/shard_map/all_gather | solution.py:164
  24.4 118.9 %all-gather.9.cloned.1.call-start = ((), (), s32[]{:S(2)}) async-start(), calls=%async_computation.19 | async-start | bytes 9437184 | tf_op jit(solution)/shard_map/all_gather | solution.py:234
  27.2 370.8 %all-gather.13.cloned.1.call-start = ((), (), s32[]{:S(2)}) async-start(), calls=%async_computation.21 | async-start | bytes 8650752 | tf_op jit(solution)/shard_map/all_gather | solution.py:230
  29.1 18.4 %all-to-all-start.4 = ((bf16[64,8,1024]{2,0,1:T(8,128)(2,1)}), bf16[64,8,1024]{2,0,1:T(8,128)(2,1)S(1)}, u32[]{:S(2)}, u32[]{:S(2)}) async-start(bf16[64,8,1024]{2,0,1:T(8,128)(2,1)} %bitcast.161), calls=%async_computation.4 | async-start | bytes 2097152 | tf_op jit(solution)/shard_map/all_to_all | solution.py:157
  47.5 111.8 %all-to-all-start.5 = ((bf16[64,8,1024]{2,0,1:T(8,128)(2,1)}), bf16[64,8,1024]{2,0,1:T(8,128)(2,1)S(1)}, u32[]{:S(2)}, u32[]{:S(2)}) async-start(bf16[64,8,1024]{2,0,1:T(8,128)(2,1)} %bitcast.208), calls=%async_computation.5 | async-start | bytes 2097152 | tf_op jit(solution)/shard_map/all_to_all | solution.py:157
  51.1 358.0 %all-gather.17.cloned.1.call-start = ((), (), s32[]{:S(2)}) async-start(), calls=%async_computation.23 | async-start | bytes 5242880 | tf_op jit(solution)/shard_map/all_gather | solution.py:164
  159.3 106.1 %all-to-all-start.1 = ((bf16[4,512,768]{1,2,0:T(8,128)(2,1)}), bf16[4,512,768]{1,2,0:T(8,128)(2,1)}, u32[]{:S(2)}, u32[]{:S(2)}) async-start(bf16[4,512,768]{1,2,0:T(8,128)(2,1)} %copy.155), calls=%async_computation.1 | async-start | bytes 6291456 | tf_op jit(solution)/shard_map/all_to_all | solution.py:246
  164.4 279.6 %all-gather.19.cloned.1.call-start = ((), (), s32[]{:S(2)}) async-start(), calls=%async_computation.24 | async-start | bytes 5242880 | tf_op jit(solution)/shard_map/all_gather | solution.py:164
  174.8 362.6 %all-gather.15.cloned.1.call-start = ((), (), s32[]{:S(2)}) async-start(), calls=%async_computation.22 | async-start | bytes 18874368 | tf_op jit(solution)/shard_map/all_gather | solution.py:205
  337.5 60.5 %copy-start.26 = (s32[2048]{0:T(1024)}, s32[2048]{0:T(1024)S(1)}, u32[]{:S(2)}) copy-start(s32[2048]{0:T(1024)S(1)} %get-tuple-element.682) | copy-start | bytes 24580
  337.5 60.5 %copy-start.44 = (f32[2048]{0:T(1024)S(1)}, f32[2048]{0:T(1024)}, u32[]{:S(2)}) copy-start(f32[2048]{0:T(1024)} %param.28) | copy-start | bytes 24580
  408.3 266.8 %reduce-scatter.10.cloned.1.call-start = ((), (), s32[]{:S(2)}) async-start(), calls=%async_computation.26 | async-start | bytes 9437184 | tf_op jit(solution)/shard_map/reduce_scatter | solution.py:280
  603.7 146.6 %reduce-scatter.8.cloned.1.call-start = ((), (), s32[]{:S(2)}) async-start(), calls=%async_computation.25 | async-start | bytes 9437184 | tf_op jit(solution)/shard_map/reduce_scatter | solution.py:284
  618.1 455.7 %reduce-scatter.18.cloned.1.call-start = ((), (), s32[]{:S(2)}) async-start(), calls=%async_computation.30 | async-start | bytes 5242880 | tf_op jit(solution)/shard_map/reduce_scatter | solution.py:176
  634.0 116.2 %copy-start.21 = (bf16[256,2048]{1,0:T(8,128)(2,1)S(1)}, bf16[256,2048]{1,0:T(8,128)(2,1)}, u32[]{:S(2)}) copy-start(bf16[256,2048]{1,0:T(8,128)(2,1)} %param.37) | copy-start | bytes 3145732
  634.0 116.2 %copy-start.49 = (f32[2048]{0:T(1024)S(1)}, f32[2048]{0:T(1024)}, u32[]{:S(2)}) copy-start(f32[2048]{0:T(1024)} %param.34) | copy-start | bytes 24580
  762.4 19.2 %all-to-all-start.6 = ((bf16[8,256,256]{2,1,0:T(8,128)(2,1)}), bf16[8,256,256]{2,1,0:T(8,128)(2,1)}, u32[]{:S(2)}, u32[]{:S(2)}) async-start(bf16[8,256,256]{2,1,0:T(8,128)(2,1)} %bitcast.159), calls=%async_computation.8 | async-start | bytes 2097152 | tf_op jit(solution)/shard_map/all_to_all | solution.py:292
  781.6 56.5 %all-to-all-start.7 = ((bf16[4,512,256]{2,1,0:T(8,128)(2,1)}), bf16[4,512,256]{2,1,0:T(8,128)(2,1)S(1)}, u32[]{:S(2)}, u32[]{:S(2)}) async-start(bf16[4,512,256]{2,1,0:T(8,128)(2,1)} %bitcast.41), calls=%async_computation.9 | async-start | bytes 2097152 | tf_op jit(solution)/shard_map/all_to_all | solution.py:299
  786.8 290.7 %reduce-scatter.20.cloned.1.call-start = ((), (), s32[]{:S(2)}) async-start(), calls=%async_computation.31 | async-start | bytes 5242880 | tf_op jit(solution)/shard_map/reduce_scatter | solution.py:176
  802.4 312.7 %reduce-scatter.14.cloned.1.call-start = ((), (), s32[]{:S(2)}) async-start(), calls=%async_computation.28 | async-start | bytes 3932160 | tf_op jit(solution)/shard_map/reduce_scatter | solution.py:176
  1055.6 250.5 %reduce-scatter.16.cloned.1.call-start = ((), (), s32[]{:S(2)}) async-start(), calls=%async_computation.29 | async-start | bytes 8650752 | tf_op jit(solution)/shard_map/reduce_scatter | solution.py:342
  1062.3 318.3 %reduce-scatter.12.cloned.1.call-start = ((), (), s32[]{:S(2)}) async-start(), calls=%async_computation.27 | async-start | bytes 9437184 | tf_op jit(solution)/shard_map/reduce_scatter | solution.py:313
  1073.8 18.4 %all-to-all-start.10 = ((bf16[8,64,1024]{2,1,0:T(8,128)(2,1)}), bf16[8,64,1024]{2,1,0:T(8,128)(2,1)S(1)}, u32[]{:S(2)}, u32[]{:S(2)}) async-start(bf16[8,64,1024]{2,1,0:T(8,128)(2,1)} %bitcast.230), calls=%async_computation.16 | async-start | bytes 2097152 | tf_op jit(solution)/shard_map/all_to_all | solution.py:177
  1093.2 18.4 %all-to-all-start.11 = ((bf16[8,64,1024]{2,1,0:T(8,128)(2,1)}), bf16[8,64,1024]{2,1,0:T(8,128)(2,1)S(1)}, u32[]{:S(2)}, u32[]{:S(2)}) async-start(bf16[8,64,1024]{2,1,0:T(8,128)(2,1)} %bitcast.231), calls=%async_computation.18 | async-start | bytes 2097152 | tf_op jit(solution)/shard_map/all_to_all | solution.py:177
  1115.2 27.8 %all-to-all-start.9 = ((bf16[8,64,768]{2,1,0:T(8,128)(2,1)}), bf16[8,64,768]{2,1,0:T(8,128)(2,1)}, u32[]{:S(2)}, u32[]{:S(2)}) async-start(bf16[8,64,768]{2,1,0:T(8,128)(2,1)} %bitcast.236), calls=%async_computation.13 | async-start | bytes 1572864 | tf_op jit(solution)/shard_map/all_to_all | solution.py:177
  1119.4 396.7 %all-reduce.3.cloned.1.call-start = ((), (), s32[]{:S(2)}) async-start(), calls=%async_computation.32 | async-start | bytes 196608 | tf_op jit(solution)/shard_map/psum | solution.py:326
  1121.2 259.4 %copy-start.10 = (bf16[256,2048]{1,0:T(8,128)(2,1)S(1)}, bf16[256,2048]{1,0:T(8,128)(2,1)}, u32[]{:S(2)}) copy-start(bf16[256,2048]{1,0:T(8,128)(2,1)} %param.21) | copy-start | bytes 3145732
  1121.2 259.4 %copy-start.30 = (f32[2048]{0:T(1024)S(1)}, f32[2048]{0:T(1024)}, u32[]{:S(2)}) copy-start(f32[2048]{0:T(1024)} %param.22) | copy-start | bytes 24580
  1121.2 259.4 %copy-start.36 = (f32[256]{0:T(256)S(1)}, f32[256]{0:T(256)}, u32[]{:S(2)}) copy-start(f32[256]{0:T(256)} %copy-done.35) | copy-start | bytes 3076
  1121.2 259.4 %copy-start.40 = (f32[256]{0:T(256)S(1)}, f32[256]{0:T(256)}, u32[]{:S(2)}) copy-start(f32[256]{0:T(256)} %copy-done.39) | copy-start | bytes 3076
  1124.2 259.3 %copy-start.34 = (f32[2048]{0:T(1024)}, f32[2048]{0:T(1024)S(1)}, u32[]{:S(2)}) copy-start(f32[2048]{0:T(1024)S(1)} %dynamic_update_slice.21) | copy-start | bytes 24580
  1124.4 259.0 %copy-start.33 = (f32[2048]{0:T(1024)}, f32[2048]{0:T(1024)S(1)}, u32[]{:S(2)}) copy-start(f32[2048]{0:T(1024)S(1)} %dynamic_update_slice.22) | copy-start | bytes 24580
  (48 other events, 831.8 us)
Sparse Core Ops, SparseCore 0:
  24.5 60.9 all-gather.10
  87.9 55.3 all-gather.8
  146.3 122.2 all-gather.12
  270.6 84.8 all-gather.16
  357.0 87.0 all-gather.18
  446.4 91.0 all-gather.14
  603.8 71.2 reduce-scatter.9
  678.9 71.2 reduce-scatter.7
  752.5 99.2 reduce-scatter.17
  854.0 75.8 reduce-scatter.19
  1055.7 59.4 reduce-scatter.13
  1117.3 188.6 reduce-scatter.15
  1309.5 71.0 reduce-scatter.11
  1389.1 126.9 all-reduce.2
